TPU v7x, 32 devices: a whole 2x2x4 slice. The times are simulated.
32 devices in a mesh: rep: 1, dp: 32 (over x, y, z, core).
Axes of the slice: x: 2, y: 2, z: 4, core: 2. Of those that a mesh axis runs over, the one named last changes fastest.
Arguments:
- x: bfloat16 [32, 2048, 640], P(('rep', 'dp'))
- dy: bfloat16 [32, 2048, 640], P(('rep', 'dp'))
- w_gate: bfloat16 [2, 640, 2048], P(None, 'dp')
- w_up: bfloat16 [2, 640, 2048], P(None, 'dp')
- w_down: bfloat16 [2, 2048, 640], P(None, 'dp')
Outputs:
- output 1: bfloat16 [32, 2048, 640], P(('rep', 'dp'))
- output 2: bfloat16 [2, 640, 2048], P('rep', 'dp')
- output 3: bfloat16 [2, 640, 2048], P('rep', 'dp')
- output 4: bfloat16 [2, 2048, 640], P('rep', 'dp')
All inputs are finite; a program needn't handle non-finite values.
Results may differ from a plain program's by a relative error of at most 0.018.
Values are sent between devices in bfloat16 or wider.
A program may use at most 2 GiB of HBM per device.

v0:
```python
import jax
import jax.numpy as jnp
from jax import lax

NAMES = ("w_gate", "w_up", "w_down")


def matmul(a, w):
    return jnp.dot(a, w, preferred_element_type=jnp.float32).astype(jnp.bfloat16)


def normed(h):
    wide = h.astype(jnp.float32)
    scale = lax.rsqrt(jnp.mean(wide**2, -1, keepdims=True) + 1e-6)
    return (wide * scale).astype(jnp.bfloat16)


def layer(h, w):
    a = normed(h)
    gate = jnp.dot(a, w["w_gate"], preferred_element_type=jnp.float32)
    up = jnp.dot(a, w["w_up"], preferred_element_type=jnp.float32)
    return h + matmul((jax.nn.silu(gate) * up).astype(jnp.bfloat16), w["w_down"])


def stack(weights, h):
    for number in range(weights["w_gate"].shape[0]):
        h = layer(h, {name: w[number] for name, w in weights.items()})
    return h


def solution(mesh):
    groups = mesh.shape["rep"]

    def step(x, dy, *weights):
        shape = x.shape
        x, dy = (t.reshape(groups, -1, *t.shape[1:]) for t in (x, dy))

        def of_a_group(x, dy):
            _, back = jax.vjp(stack, dict(zip(NAMES, weights, strict=True)), x)
            by_weights, by_x = back(dy)
            return (by_x, *(by_weights[name] for name in NAMES))

        by_x, *by_weights = jax.vmap(of_a_group)(x, dy)
        return (by_x.reshape(shape), *(t.reshape(-1, *t.shape[2:]) for t in by_weights))

    return step
```

profile of v0, /device:TPU:0, one launch (start us, length us, event | category | flops | bytes accessed | tf_op | source)
XLA Modules:
  0.0 1690.5 jit_solution(3562762078606018020)
XLA Ops:
  32.2 157.1 %while.13 = (bf16[1,2048,640]{2,1,0:T(8,128)(2,1)S(1)}, bf16[1,64,640]{2,1,0:T(8,128)(2,1)S(1)}, bf16[1,2048,2048]{1,2,0:T(8,128)(2,1)}, bf16[1,64,640]{2,1,0:T(...) while((bf16[1,2048,640]{2,1,0:T(8,128)(2,1)S(1)}, ...), condition=%wide.windowed_dot_general_cond_ag, body=%wide.windowed_dot_general_body_ag.sunk | while | flops 671252480 | bytes 10027549 | solution.py:9
  32.2 6.4 collective-permute-start
  61.3 5.6 collective-permute-done.2
  98.2 6.1 collective-permute-done.2
  117.9 5.8 collective-permute-done.2
  137.4 6.0 collective-permute-done.2
  189.3 12.1 copy.24
  201.3 13.6 fusion.222
  215.0 19.5 %fusion.176 = (bf16[1,2048,2048]{2,1,0:T(8,128)(2,1)}, f32[2048,2048]{1,0:T(8,128)}) fusion(f32[2048,2048]{1,0:T(8,128)} %fusion.222, bf16[1,640,2048]{2,0,1:T(2,128)(2,1)} %all-gather.29.cloned.1.call-done, bf16[1,2048,640]{1,2,0:T(8,128)(2,1)} %fusion.187), kind=kOutput, calls=%fused_computation.215 | convolution fusion | flops 5393874944 | bytes 47185920 | tf_op jit(solution)/vmap(jvp())/dot_general | solution.py:21
  234.5 12.3 copy.28
  246.8 9.6 fusion.189
  260.2 19.7 %all-gather.33.cloned.1.call-done = bf16[1,640,2048]{2,0,1:T(2,128)(2,1)} async-done(((bf16[1,20,2048]{2,0,1:T(2,128)(2,1)}), bf16[1,640,2048]{2,0,1:T(2,128)(2,1)}) %all-gather.33.cloned.1.call-update) | async-done | bytes 2621456 | tf_op jit(solution)/vmap(jvp())/squeeze | solution.py:27
  279.9 13.8 fusion.216
  293.7 53.8 %all-gather.35.cloned.1.call-done = bf16[1,640,2048]{2,0,1:T(2,128)(2,1)} async-done(((bf16[1,20,2048]{2,0,1:T(2,128)(2,1)}), bf16[1,640,2048]{2,0,1:T(2,128)(2,1)}) %all-gather.35.cloned.1.call-update) | async-done | bytes 2621456 | tf_op jit(solution)/vmap(jvp())/squeeze | solution.py:27
  347.5 19.0 %fusion.170 = (bf16[1,2048,2048]{2,1,0:T(8,128)(2,1)}, f32[2048,2048]{1,0:T(8,128)}) fusion(f32[2048,2048]{1,0:T(8,128)} %fusion.216, bf16[1,640,2048]{2,0,1:T(2,128)(2,1)} %all-gather.35.cloned.1.call-done, bf16[1,2048,640]{1,2,0:T(8,128)(2,1)} %fusion.190), kind=kOutput, calls=%fused_computation.205 | convolution fusion | flops 5393874944 | bytes 47185920 | tf_op jit(solution)/vmap(jvp())/dot_general | solution.py:21
  366.5 12.4 copy.26
  378.9 167.2 %while.18 = (bf16[1,2048,2048]{1,2,0:T(8,128)(2,1)}, bf16[1,2048,640]{2,1,0:T(8,128)(2,1)S(1)}, f32[64,640]{1,0:T(8,128)S(1)}, f32[64,640]{1,0:T(8,128)}, u32[]{...) while((bf16[1,2048,2048]{1,2,0:T(8,128)(2,1)}, ...), condition=%wide.windowed_dot_general_cond_rs.4.clone, body=%wide.windowed_dot_general_body_rs.4.clone.sunk | while | flops 673431552 | bytes 61473388 | solution.py:9
  546.1 15.9 fusion.161
  562.1 14.6 fusion.195
  576.7 10.3 fusion.191
  591.9 166.4 %while.19 = (bf16[1,2048,640]{2,1,0:T(8,128)(2,1)}, bf16[1,2048,2048]{1,2,0:T(8,128)(2,1)}, f32[640,64]{0,1:T(8,128)S(1)}, f32[640,64]{0,1:T(8,128)}, u32[]{:T(1...) while((bf16[1,2048,640]{2,1,0:T(8,128)(2,1)}, ...), condition=%wide.windowed_dot_general_cond_rs.5.clone, body=%wide.windowed_dot_general_body_rs.5.clone.sunk | while | flops 673431552 | bytes 71959176 | solution.py:9
  758.9 203.6 %while.16 = (bf16[1,2048,2048]{2,1,0:T(8,128)(2,1)}, bf16[1,2048,640]{1,2,0:T(8,128)(2,1)S(1)}, f32[2048,20]{0,1:T(8,128)S(1)}, f32[2048,20]{0,1:T(8,128)}, u32[...) while((bf16[1,2048,2048]{2,1,0:T(8,128)(2,1)}, ...), condition=%wide.windowed_dot_general_cond_rs.2.clone, body=%wide.windowed_dot_general_body_rs.2.clone.sunk | while | flops 671989760 | bytes 27918928 | solution.py:21
  771.5 5.5 collective-permute-start.15
  797.1 5.5 collective-permute-start.15
  822.6 5.5 collective-permute-start.15
  963.2 24.7 %fusion.163 = (bf16[1,2048,2048]{2,1,0:T(8,128)(2,1)}, bf16[1,2048,2048]{2,1,0:T(8,128)(2,1)}) fusion(f32[2048,2048]{1,0:T(8,128)} %fusion.222, f32[2048,2048]{1,0:T(8,128)} %get-tuple-element.310, bf16[1,2048,640]{2,1,0:T(8,128)(2,1)} %all-gather.31.cloned.1.call-done, bf16[1,2048,640]{1,2,0:T(8,128)(2,1)} %copy-done.9), kind=kOutput, calls=%fused_computation.197 | convolution fusion | flops 5435817984 | bytes 55574528 | tf_op jit(solution)/vmap(transpose(jvp()))/dot_general | solution.py:9
  987.9 218.8 %while.17 = (bf16[1,2048,2048]{2,1,0:T(8,128)(2,1)}, bf16[1,2048,640]{1,2,0:T(8,128)(2,1)S(1)}, f32[2048,20]{0,1:T(8,128)S(1)}, f32[2048,20]{0,1:T(8,128)}, u32[...) while((bf16[1,2048,2048]{2,1,0:T(8,128)(2,1)}, ...), condition=%wide.windowed_dot_general_cond_rs.3.clone, body=%wide.windowed_dot_general_body_rs.3.clone.sunk | while | flops 671989760 | bytes 28574316 | solution.py:21
  1207.4 218.8 %while.14 = (bf16[1,2048,2048]{2,1,0:T(8,128)(2,1)}, bf16[1,2048,640]{1,2,0:T(8,128)(2,1)}, f32[2048,20]{0,1:T(8,128)S(1)}, f32[2048,20]{0,1:T(8,128)}, u32[]{:T...) while((bf16[1,2048,2048]{2,1,0:T(8,128)(2,1)}, ...), condition=%wide.windowed_dot_general_cond_rs.clone, body=%wide.windowed_dot_general_body_rs.clone.sunk | while | flops 671989760 | bytes 28574316 | solution.py:20
  1426.2 219.5 %while.15 = (bf16[1,2048,2048]{2,1,0:T(8,128)(2,1)}, bf16[1,2048,640]{1,2,0:T(8,128)(2,1)S(1)}, f32[2048,20]{0,1:T(8,128)S(1)}, f32[2048,20]{0,1:T(8,128)}, u32[...) while((bf16[1,2048,2048]{2,1,0:T(8,128)(2,1)}, ...), condition=%wide.windowed_dot_general_cond_rs.1.clone, body=%wide.windowed_dot_general_body_rs.1.clone.sunk | while | flops 671989760 | bytes 28574316 | solution.py:20
  1645.8 11.5 fusion.201
  1657.4 6.9 fusion.188
  1670.7 7.3 collective-permute-done.29
  (1006 shorter events, 1349.7 us)
Async XLA Ops:
  7.2 194.2 %all-gather.27.cloned.1.call-start = ((), (), s32[]{:S(2)}) async-start(), calls=%async_computation | async-start | bytes 5406720 | tf_op jit(solution)/vmap(jvp())/squeeze | solution.py:27
  9.2 205.7 %all-gather.29.cloned.1.call-start = ((), (), s32[]{:S(2)}) async-start(), calls=%async_computation.1 | async-start | bytes 5406720 | tf_op jit(solution)/vmap(jvp())/squeeze | solution.py:27
  11.3 235.5 %all-gather.31.cloned.1.call-start = ((), (), s32[]{:S(2)}) async-start(), calls=%async_computation.2 | async-start | bytes 2703360 | tf_op jit(solution)/vmap(jvp())/squeeze | solution.py:27
  13.0 266.9 %all-gather.33.cloned.1.call-start = ((), (), s32[]{:S(2)}) async-start(), calls=%async_computation.3 | async-start | bytes 5406720 | tf_op jit(solution)/vmap(jvp())/squeeze | solution.py:27
  13.5 333.9 %all-gather.35.cloned.1.call-start = ((), (), s32[]{:S(2)}) async-start(), calls=%async_computation.4 | async-start | bytes 5406720 | tf_op jit(solution)/vmap(jvp())/squeeze | solution.py:27
  13.6 14.2 collective-permute-start.28
  546.1 1134.9 %collective-permute-start.33 = (f32[64,640]{1,0:T(8,128)}, f32[64,640]{1,0:T(8,128)}, u32[]{:S(2)}, u32[]{:S(2)}) collective-permute-start(f32[64,640]{1,0:T(8,128)} %get-tuple-element.52), channel_id=46, source_target_pairs={{0,1},{1,2},{2,3},{3,4},{4,5},{5,6},{6,7},{7,8},{8,9},{9,10},{10,1... | collective-permute-start | bytes 491528 | tf_op jit(solution)/vmap(transpose(jvp()))/dot_general | solution.py:9
  758.3 923.8 %collective-permute-start.34 = (f32[640,64]{0,1:T(8,128)}, f32[640,64]{0,1:T(8,128)}, u32[]{:S(2)}, u32[]{:S(2)}) collective-permute-start(f32[640,64]{0,1:T(8,128)} %get-tuple-element.54), channel_id=52, source_target_pairs={{0,1},{1,2},{2,3},{3,4},{4,5},{5,6},{6,7},{7,8},{8,9},{9,10},{10,1... | collective-permute-start | bytes 491528 | tf_op jit(solution)/vmap(transpose(jvp()))/dot_general | solution.py:9
  962.5 706.2 %collective-permute-start.31 = (f32[2048,20]{0,1:T(8,128)}, f32[2048,20]{0,1:T(8,128)}, u32[]{:S(2)}, u32[]{:S(2)}) collective-permute-start(f32[2048,20]{0,1:T(8,128)} %get-tuple-element.48), channel_id=34, source_target_pairs={{0,1},{1,2},{2,3},{3,4},{4,5},{5,6},{6,7},{7,8},{8,9},{9,10},{10,1... | collective-permute-start | bytes 491528 | tf_op jit(solution)/vmap(transpose(jvp()))/dot_general | solution.py:21
  1001.3 11.4 collective-permute-start.19
  1028.8 11.4 collective-permute-start.19
  1056.3 11.4 collective-permute-start.19
  1083.7 11.4 collective-permute-start.19
  1111.2 11.4 collective-permute-start.19
  1138.7 11.4 collective-permute-start.19
  1166.1 11.4 collective-permute-start.19
  1193.6 11.4 collective-permute-start.19
  1221.0 11.2 collective-permute-start.7
  1248.5 11.2 collective-permute-start.7
  1276.0 11.2 collective-permute-start.7
  1303.4 11.2 collective-permute-start.7
  1413.2 11.2 collective-permute-start.7
  1439.8 11.4 collective-permute-start.11
  1467.3 11.4 collective-permute-start.11
  1494.9 11.4 collective-permute-start.11
  1522.4 11.4 collective-permute-start.11
  1549.9 11.4 collective-permute-start.11
  1577.4 11.4 collective-permute-start.11
  1605.0 11.4 collective-permute-start.11
  1632.5 11.4 collective-permute-start.11
  1645.7 24.0 %collective-permute-start.32 = (f32[2048,20]{0,1:T(8,128)}, f32[2048,20]{0,1:T(8,128)}, u32[]{:S(2)}, u32[]{:S(2)}) collective-permute-start(f32[2048,20]{0,1:T(8,128)} %get-tuple-element.50), channel_id=40, source_target_pairs={{0,1},{1,2},{2,3},{3,4},{4,5},{5,6},{6,7},{7,8},{8,9},{9,10},{10,1... | collective-permute-start | bytes 491528 | tf_op jit(solution)/vmap(transpose(jvp()))/dot_general | solution.py:21
  1668.8 11.4 collective-permute-start.30
  (284 other events, 3227.0 us)
Sparse Core Ops, SparseCore 0:
  11.4 69.1 all-gather.26
  83.5 67.4 all-gather.28
  153.8 58.5 all-gather.30
  215.7 64.1 all-gather.32
  283.2 64.2 all-gather.34
where the time goes:
time: 1700 us; the launch traced here: 1690 us
  starting transfers between devices  533 us (31%)
  matrix products  519 us (31%)
  waiting for transfers between devices  286 us (17%)
  other arithmetic  231 us (14%)
  local copies, waits for them, and re-layouts  104 us (6%)
    dot_general x36, matrix products, layer(): up = jnp.dot(a, w['w_up'], preferred_element_type=jnp.float32)  221 us
    dot_general x36, matrix products, layer(): gate = jnp.dot(a, w['w_gate'], preferred_element_type=jnp.float32)  204 us
    dot_general x99, waiting for transfers between devices, matmul(): jnp.dot(a, w, preferred_element_type=jnp.float32).astype(jnp.bfloat16)  193 us
    dot_general x99, starting transfers between devices, matmul(): jnp.dot(a, w, preferred_element_type=jnp.float32).astype(jnp.bfloat16)  189 us
    dot_general x66, starting transfers between devices, layer(): up = jnp.dot(a, w['w_up'], preferred_element_type=jnp.float32)  173 us
    dot_general x66, starting transfers between devices, layer(): gate = jnp.dot(a, w['w_gate'], preferred_element_type=jnp.float32)  171 us
    dot_general x50, matrix products, matmul(): jnp.dot(a, w, preferred_element_type=jnp.float32).astype(jnp.bfloat16)  94 us
    dot_general x96, other arithmetic  83.5 us
  transfers between devices with their start and end apart: 236, of which 97 were waited for; matrix products, arithmetic and copies ran while one was open for 47% of the time, Pallas kernels for 0%

commit v1 on v0

v1 whole, which is shorter than its diff:
```python
import jax
import jax.numpy as jnp
from jax import lax
from jax.sharding import PartitionSpec as P

LAYERS, D, FF = 2, 640, 2048
F32, BF16 = jnp.float32, jnp.bfloat16


def dot(a, b, ca, cb):
    return lax.dot_general(a, b, (((ca,), (cb,)), ((), ())), preferred_element_type=F32)


def solution(mesh):
    n = mesh.shape["dp"]

    def gather(g, u, d):
        flat = jnp.concatenate([t.reshape(-1, 128) for t in (g, u, d)], 0)
        full = lax.all_gather(flat, "dp", axis=0, tiled=False)
        k = g.size // 128
        return (
            full[:, :k].reshape(D, FF),
            full[:, k : 2 * k].reshape(D, FF),
            full[:, 2 * k :].reshape(FF, D),
        )

    def scatter(g, u, d):
        flat = jnp.concatenate([t.reshape(n, -1, 128) for t in (g, u, d)], 1)
        mine = lax.psum_scatter(flat, "dp", scatter_dimension=0, tiled=False)
        k = D * FF // n // 128
        return (
            mine[:k].reshape(D // n, FF),
            mine[k : 2 * k].reshape(D // n, FF),
            mine[2 * k :].reshape(FF // n, D),
        )

    def norm(h):
        wide = h.astype(F32)
        scale = lax.rsqrt(jnp.mean(wide**2, -1, keepdims=True) + 1e-6)
        return wide, scale, (wide * scale).astype(BF16)

    def up_half(a, w):
        gate, up = dot(a, w[0], 1, 0), dot(a, w[1], 1, 0)
        s = jax.nn.sigmoid(gate)
        return gate, up, s, (gate * s * up).astype(BF16)

    def back(dh, wide, scale, a, gate, up, s, p, w):
        dp = dot(dh, w[2], 1, 1).astype(BF16).astype(F32)
        dwd = dot(p, dh, 0, 0).astype(BF16)
        dup = (dp * gate * s).astype(BF16)
        dgate = (dp * up * s * (1 + gate * (1 - s))).astype(BF16)
        dwg = dot(a, dgate, 0, 0).astype(BF16)
        dwu = dot(a, dup, 0, 0).astype(BF16)
        da = dot(dgate, w[0], 1, 1).astype(BF16) + dot(dup, w[1], 1, 1).astype(BF16)
        da = da.astype(F32)
        inner = jnp.mean(da * wide, -1, keepdims=True)
        dwide = scale * da - wide * (scale**3 * inner)
        return (dwg, dwu, dwd), dh + dwide.astype(BF16)

    def body(x, dy, wg, wu, wd):
        x, dy = x[0], dy[0]
        w0 = gather(wg[0], wu[0], wd[0])
        w1 = gather(wg[1], wu[1], wd[1])
        n0 = norm(x)
        g0 = up_half(n0[2], w0)
        h = x + dot(g0[3], w0[2], 1, 0).astype(BF16)
        n1 = norm(h)
        g1 = up_half(n1[2], w1)
        dw1, dh = back(dy, *n1, *g1, w1)
        r1 = scatter(*dw1)
        dw0, dx = back(dh, *n0, *g0, w0)
        r0 = scatter(*dw0)
        return (dx[None], *(jnp.stack([a, b]) for a, b in zip(r0, r1)))

    s = P(("rep", "dp"), None, None)
    ws = P(None, "dp", None)
    return jax.shard_map(
        body, mesh=mesh, in_specs=(s, s, ws, ws, ws), out_specs=(s, *([P("rep", "dp", None)] * 3)), check_vma=False
    )
```

time: 1700 us -> 623 us (0.37)
  starting transfers between devices: 533 us -> 0.34 us
  matrix products: 519 us -> 204 us
  other arithmetic: 231 us -> 23.2 us
    dot_general x231 -> x0, starting transfers between devices: 533 us -> none  [the longest x99 189 us: matmul(): jnp.dot(a, w, preferred_element_type=jnp.float32).astype(jnp.bfloat16)]
    dot_general x122 -> x17, matrix products: 519 us -> 204 us  [dot(): lax.dot_general(a, b, (((ca,), (cb,)), ((), ())), preferred_element_type=...]
    dot_general x231 -> x0, waiting for transfers between devices: 212 us -> none  [the longest x99 193 us: matmul(): jnp.dot(a, w, preferred_element_type=jnp.float32).astype(jnp.bfloat16)]
    dot_general x192 -> x0, other arithmetic: 198 us -> none
    reduce_scatter x0 -> x2, waiting for transfers between devices: none -> 142 us  [scatter(): mine = lax.psum_scatter(flat, 'dp', scatter_dimension=0, tiled=False)]
    all_gather x0 -> x2, waiting for transfers between devices: none -> 134 us  [gather(): full = lax.all_gather(flat, 'dp', axis=0, tiled=False)]
    squeeze x5 -> x0, waiting for transfers between devices: 73.5 us -> none  [stack(): h = layer(h, {name: w[number] for name, w in weights.items()})]
    reshape x0 -> x12, local copies, waits for them, and re-layouts: none -> 62.8 us  [the longest x6 31.1 us: scatter(): flat = jnp.concatenate([t.reshape(n, -1, 128) for t in (g, u, d)], 1)]
  transfers between devices with their start and end apart: 236 -> 4, of which waited for: 97 -> 4; matrix products, arithmetic and copies ran while one was open for 47% -> 20% of each run, Pallas kernels for 0% -> 0%
where the time goes in v1:
time: 623 us; the launch traced here: 618 us
  waiting for transfers between devices  276 us (44%)
  matrix products  204 us (33%)
  local copies, waits for them, and re-layouts  101 us (16%)
  other arithmetic  23.2 us (4%)
  between operations  14.4 us (2%)
    dot_general x17, matrix products, dot(): lax.dot_general(a, b, (((ca,), (cb,)), ((), ())), preferred_element_type=...  204 us
    reduce_scatter x2, waiting for transfers between devices, scatter(): mine = lax.psum_scatter(flat, 'dp', scatter_dimension=0, tiled=False)  142 us
    all_gather x2, waiting for transfers between devices, gather(): full = lax.all_gather(flat, 'dp', axis=0, tiled=False)  134 us
    reshape x6, local copies, waits for them, and re-layouts, scatter(): flat = jnp.concatenate([t.reshape(n, -1, 128) for t in (g, u, d)], 1)  31.1 us
    unnamed x51, local copies, waits for them, and re-layouts  19.6 us
    concatenate x2, other arithmetic, scatter(): flat = jnp.concatenate([t.reshape(n, -1, 128) for t in (g, u, d)], 1)  12.6 us
  transfers between devices with their start and end apart: 4, of which 4 were waited for; matrix products, arithmetic and copies ran while one was open for 20% of the time, Pallas kernels for 0%

profile of v1, /device:TPU:0, one launch (start us, length us, event | category | flops | bytes accessed | tf_op | source)
XLA Modules:
  0.0 618.4 jit_solution(9894734661375067311)
XLA Ops:
  23.0 67.5 %all-gather.7.cloned.1.call-done = bf16[30720,128]{1,0:T(8,128)(2,1)} async-done(((bf16[960,128]{1,0:T(8,128)(2,1)}), bf16[30720,128]{1,0:T(8,128)(2,1)}) %all-gather.7.cloned.1.call-update) | async-done | bytes 7864336 | tf_op jit(solution)/shard_map/all_gather | solution.py:19
  90.5 5.5 fusion.45
  101.2 66.2 %all-gather.5.cloned.1.call-done = bf16[30720,128]{1,0:T(8,128)(2,1)} async-done(((bf16[960,128]{1,0:T(8,128)(2,1)}), bf16[30720,128]{1,0:T(8,128)(2,1)}) %all-gather.5.cloned.1.call-update) | async-done | bytes 7864336 | tf_op jit(solution)/shard_map/all_gather | solution.py:19
  167.4 5.6 fusion.46
  173.0 5.5 reshape.114
  194.0 5.5 reshape.115
  199.5 11.2 %convolution_convert_fusion = bf16[2048,2048]{0,1:T(8,128)(2,1)} fusion(bf16[2048,640]{1,0:T(8,128)(2,1)} %reshape.115, bf16[1,2048,640]{2,1,0:T(8,128)(2,1)} %param.6), kind=kOutput, calls=%fused_computation.29 | convolution fusion | flops 5372903424 | bytes 13631488 | tf_op jit(solution)/shard_map/dot_general | solution.py:11
  210.7 9.9 %fusion.40 = f32[2048,2048]{1,0:T(8,128)} fusion(bf16[640,2048]{1,0:T(8,128)(2,1)S(1)} %copy-done.9, bf16[1,2048,640]{2,1,0:T(8,128)(2,1)S(1)} %copy-done.7, f32[2048]{0:T(1024)S(1)} %add_rsqrt_fusion.1), kind=kOutput, calls=%fused_computation.67 | convolution fusion | flops 5372641280 | bytes 22028288 | tf_op jit(solution)/shard_map/dot_general | solution.py:11
  220.7 18.6 %multiply_convert_fusion.1 = (bf16[2048,2048]{1,0:T(8,128)(2,1)}, f32[2048,2048]{1,0:T(8,128)}) fusion(f32[2048,2048]{1,0:T(8,128)} %fusion.40, bf16[640,2048]{1,0:T(8,128)(2,1)} %reshape.113, bf16[1,2048,640]{2,1,0:T(8,128)(2,1)S(1)} %copy-done.7, f32[2048]{0:T(1024)S(1)} %add_rsqrt_fusion.1), kind=kOutput, calls=%fused_computation.16 | convolution fusion | flops 5397807104 | bytes 47194112 | tf_op jit(solution)/shard_map/dot_general | solution.py:11
  239.3 9.5 %fusion.18 = (f32[2048]{0:T(1024)S(1)}, bf16[2048,640]{0,1:T(8,128)(2,1)S(1)}) fusion(bf16[2048,2048]{1,0:T(8,128)(2,1)} %get-tuple-element.34, bf16[2048,640]{1,0:T(8,128)(2,1)} %reshape.114, bf16[1,2048,640]{1,2,0:T(8,128)(2,1)S(1)} %copy.14), kind=kOutput, calls=%fused_computation.40 | convolution fusion | flops 5375260672 | bytes 16261120 | tf_op jit(solution)/shard_map/dot_general | solution.py:11
  248.9 10.3 %fusion.34 = f32[2048,2048]{1,0:T(8,128)} fusion(bf16[640,2048]{1,0:T(8,128)(2,1)S(1)} %copy-done.13, bf16[2048,640]{0,1:T(8,128)(2,1)S(1)} %get-tuple-element.37, f32[2048]{0:T(1024)S(1)} %add_rsqrt_fusion), kind=kOutput, calls=%fused_computation.64 | convolution fusion | flops 5372641280 | bytes 22028288 | tf_op jit(solution)/shard_map/dot_general | solution.py:11
  259.1 21.8 %fusion.7 = (bf16[2048,2048]{1,0:T(8,128)(2,1)}, bf16[2048,2048]{1,0:T(8,128)(2,1)}, f32[2048,2048]{1,0:T(8,128)}) fusion(bf16[2048,2048]{0,1:T(8,128)(2,1)S(1)} %copy-done.19, f32[2048,2048]{1,0:T(8,128)} %fusion.34, bf16[640,2048]{1,0:T(8,128)(2,1)S(1)} %copy-done.12, bf16[2048,640]{0,1:T(8,128)(2,1)S(1)} %get-tuple-element.37, f32[2048]{0:T(1024)S(1)} %add_rsqrt_fusion), kind=kOutput, calls=%fused_computation.11 | convolution fusion | flops 5431361536 | bytes 63971328 | tf_op jit(solution)/shard_map/dot_general | solution.py:11
  280.9 11.0 %convolution_convert_fusion.9 = bf16[2048,640]{0,1:T(8,128)(2,1)} fusion(bf16[2048,2048]{1,0:T(8,128)(2,1)} %get-tuple-element.19, bf16[640,2048]{1,0:T(8,128)(2,1)S(1)} %copy-done.12), kind=kOutput, calls=%fused_computation.52 | convolution fusion | flops 5370019840 | bytes 13631488 | tf_op jit(solution)/shard_map/dot_general | solution.py:11
  291.9 7.0 %convolution_convert_fusion.2 = bf16[640,2048]{1,0:T(8,128)(2,1)} fusion(bf16[2048,2048]{1,0:T(8,128)(2,1)S(1)} %copy-done.20, bf16[2048,640]{0,1:T(8,128)(2,1)S(1)} %get-tuple-element.37, f32[2048]{0:T(1024)S(1)} %add_rsqrt_fusion), kind=kOutput, calls=%fused_computation.45 | convolution fusion | flops 5373952000 | bytes 13639680 | tf_op jit(solution)/shard_map/dot_general | solution.py:11
  298.9 15.7 %fusion.21 = bf16[2048,640]{1,0:T(8,128)(2,1)} fusion(f32[2048,2048]{1,0:T(8,128)} %get-tuple-element.38, f32[2048,2048]{1,0:T(8,128)} %fusion.34, bf16[1,2048,640]{2,1,0:T(8,128)(2,1)S(1)} %copy-done.8), kind=kOutput, calls=%fused_computation.44 | convolution fusion | flops 5395185664 | bytes 38797312 | tf_op jit(solution)/shard_map/dot_general | solution.py:11
  318.9 10.8 %convolution_convert_fusion.3 = bf16[640,2048]{1,0:T(8,128)(2,1)} fusion(bf16[2048,2048]{1,0:T(8,128)(2,1)} %get-tuple-element.18, bf16[2048,640]{0,1:T(8,128)(2,1)} %copy-done.5, f32[2048]{0:T(1024)S(1)} %add_rsqrt_fusion), kind=kOutput, calls=%fused_computation.46 | convolution fusion | flops 5373952000 | bytes 13639680 | tf_op jit(solution)/shard_map/dot_general | solution.py:11
  329.7 11.0 %fusion.20 = (f32[2048]{0:T(1024)S(1)}, bf16[2048,640]{0,1:T(8,128)(2,1)}) fusion(bf16[2048,640]{0,1:T(8,128)(2,1)S(1)} %copy-done.6, bf16[2048,640]{0,1:T(8,128)(2,1)S(1)} %copy-done.22, bf16[2048,2048]{1,0:T(8,128)(2,1)} %get-tuple-element.18, bf16[640,2048]{1,0:T(8,128)(2,1)S(1)} %copy-done.14), kind=kOutput, calls=%fused_computation.42 | convolution fusion | flops 5376571392 | bytes 18882560 | tf_op jit(solution)/shard_map/dot_general | solution.py:11
  340.7 5.3 reshape.121
  345.9 5.3 reshape.122
  351.2 6.0 pad_maximum_fusion.1
  363.4 20.0 %fusion.2 = (bf16[2048,2048]{1,0:T(8,128)(2,1)S(1)}, bf16[2048,2048]{1,0:T(8,128)(2,1)}) fusion(f32[2048,2048]{1,0:T(8,128)} %get-tuple-element.35, f32[2048,2048]{1,0:T(8,128)} %fusion.40, bf16[2048,640]{0,1:T(8,128)(2,1)S(1)} %fusion.25, bf16[2048,640]{1,0:T(8,128)(2,1)S(1)} %copy-done.11), kind=kOutput, calls=%fused_computation.4 | convolution fusion | flops 5431623680 | bytes 55574528 | tf_op jit(solution)/shard_map/dot_general | solution.py:11
  386.6 7.1 %convolution_convert_fusion.6 = bf16[640,2048]{1,0:T(8,128)(2,1)} fusion(bf16[2048,2048]{1,0:T(8,128)(2,1)S(1)} %get-tuple-element.16, bf16[1,2048,640]{1,2,0:T(8,128)(2,1)S(1)} %copy-done.1, f32[2048]{0:T(1024)S(1)} %copy-done.18), kind=kOutput, calls=%fused_computation.49 | convolution fusion | flops 5373952000 | bytes 13639680 | tf_op jit(solution)/shard_map/dot_general | solution.py:11
  393.7 5.3 reshape.118
  399.0 10.2 %convolution_convert_fusion.5 = bf16[640,2048]{1,0:T(8,128)(2,1)} fusion(bf16[2048,2048]{1,0:T(8,128)(2,1)} %get-tuple-element.17, bf16[1,2048,640]{1,2,0:T(8,128)(2,1)S(1)} %copy-done.1, f32[2048]{0:T(1024)S(1)} %copy-done.18), kind=kOutput, calls=%fused_computation.48 | convolution fusion | flops 5373952000 | bytes 13639680 | tf_op jit(solution)/shard_map/dot_general | solution.py:11
  409.2 5.3 reshape.119
  414.5 11.1 %convolution_convert_fusion.4 = bf16[2048,640]{1,0:T(8,128)(2,1)} fusion(bf16[2048,2048]{1,0:T(8,128)(2,1)} %get-tuple-element.34, bf16[2048,640]{0,1:T(8,128)(2,1)} %copy-done.2), kind=kOutput, calls=%fused_computation.47 | convolution fusion | flops 5370019840 | bytes 13631488 | tf_op jit(solution)/shard_map/dot_general | solution.py:11
  425.6 5.7 reshape.120
  431.3 6.6 %pad_maximum_fusion = bf16[32,960,128]{2,1,0:T(8,128)(2,1)} fusion(bf16[32,320,128]{2,1,0:T(8,128)(2,1)} %reshape.120, bf16[32,320,128]{2,1,0:T(8,128)(2,1)} %reshape.119, bf16[32,320,128]{2,1,0:T(8,128)(2,1)} %reshape.118), kind=kLoop, calls=%fused_computation.27 | loop fusion | flops 23592960 | bytes 15728640 | tf_op jit(solution)/shard_map/concatenate | solution.py:28
  438.0 9.8 %convolution_convert_fusion.7 = bf16[2048,640]{0,1:T(8,128)(2,1)S(1)} fusion(bf16[2048,2048]{1,0:T(8,128)(2,1)} %get-tuple-element.17, bf16[640,2048]{1,0:T(8,128)(2,1)} %reshape.113), kind=kOutput, calls=%fused_computation.50 | convolution fusion | flops 5370019840 | bytes 13631488 | tf_op jit(solution)/shard_map/dot_general | solution.py:11
  447.8 8.7 %fusion.16 = (f32[2048]{0:T(1024)S(1)}, bf16[2048,640]{0,1:T(8,128)(2,1)S(1)}) fusion(bf16[1,2048,640]{1,2,0:T(8,128)(2,1)S(1)} %copy-done.1, bf16[2048,640]{0,1:T(8,128)(2,1)S(1)} %convolution_convert_fusion.7, bf16[2048,2048]{1,0:T(8,128)(2,1)} %copy-done.21, bf16[640,2048]{1,0:T(8,128)(2,1)S(1)} %copy-done.10), kind=kOutput, calls=%fused_computation.38 | convolution fusion | flops 5376571392 | bytes 18882560 | tf_op jit(solution)/shard_map/dot_general | solution.py:11
  464.3 15.4 %reduce-scatter.5.cloned.1.call-done = bf16[1,960,128]{2,1,0:T(8,128)(2,1)} async-done(((bf16[32,960,128]{2,1,0:T(8,128)(2,1)}), bf16[1,960,128]{2,1,0:T(8,128)(2,1)}) %reduce-scatter.5.cloned.1.call-update) | async-done | bytes 245776 | tf_op jit(solution)/shard_map/reduce_scatter | solution.py:29
  480.8 127.1 %reduce-scatter.3.cloned.1.call-done = bf16[1,960,128]{2,1,0:T(8,128)(2,1)} async-done(((bf16[32,960,128]{2,1,0:T(8,128)(2,1)}), bf16[1,960,128]{2,1,0:T(8,128)(2,1)}) %reduce-scatter.3.cloned.1.call-update) | async-done | bytes 245776 | tf_op jit(solution)/shard_map/reduce_scatter | solution.py:29
  (93 shorter events, 62.8 us)
Async XLA Ops:
  7.2 83.3 %all-gather.7.cloned.1.call-start = ((), (), s32[]{:S(2)}) async-start(), calls=%async_computation.5 | async-start | bytes 8110080 | tf_op jit(solution)/shard_map/all_gather | solution.py:19
  12.6 154.8 %all-gather.5.cloned.1.call-start = ((), (), s32[]{:S(2)}) async-start(), calls=%async_computation.4 | async-start | bytes 8110080 | tf_op jit(solution)/shard_map/all_gather | solution.py:19
  13.6 466.1 %reduce-scatter.5.cloned.1.call-start = ((), (), s32[]{:S(2)}) async-start(), calls=%async_computation.3 | async-start | bytes 8110080 | tf_op jit(solution)/shard_map/reduce_scatter | solution.py:29
  16.8 222.5 %copy-start = (bf16[1,2048,640]{1,2,0:T(8,128)(2,1)}, bf16[1,2048,640]{1,2,0:T(8,128)(2,1)S(1)}, u32[]{:S(2)}) copy-start(bf16[1,2048,640]{1,2,0:T(8,128)(2,1)S(1)} %copy.14) | copy-start | bytes 7864324
  22.4 0.6 copy-start.15
  23.0 197.7 %copy-start.17 = (f32[2048]{0:T(1024)}, f32[2048]{0:T(1024)S(1)}, u32[]{:S(2)}) copy-start(f32[2048]{0:T(1024)S(1)} %add_rsqrt_fusion.1) | copy-start | bytes 24580
  199.5 11.2 %copy-start.7 = (bf16[1,2048,640]{2,1,0:T(8,128)(2,1)S(1)}, bf16[1,2048,640]{2,1,0:T(8,128)(2,1)}, u32[]{:S(2)}) copy-start(bf16[1,2048,640]{2,1,0:T(8,128)(2,1)} %param.5) | copy-start | bytes 7864324
  199.5 11.2 %copy-start.9 = (bf16[640,2048]{1,0:T(8,128)(2,1)S(1)}, bf16[640,2048]{1,0:T(8,128)(2,1)}, u32[]{:S(2)}) copy-start(bf16[640,2048]{1,0:T(8,128)(2,1)} %reshape.112) | copy-start | bytes 7864324
  239.3 9.5 %copy-start.13 = (bf16[640,2048]{1,0:T(8,128)(2,1)S(1)}, bf16[640,2048]{1,0:T(8,128)(2,1)}, u32[]{:S(2)}) copy-start(bf16[640,2048]{1,0:T(8,128)(2,1)} %reshape.117) | copy-start | bytes 7864324
  248.8 43.1 %copy-start.5 = (bf16[2048,640]{0,1:T(8,128)(2,1)}, bf16[2048,640]{0,1:T(8,128)(2,1)S(1)}, u32[]{:S(2)}) copy-start(bf16[2048,640]{0,1:T(8,128)(2,1)S(1)} %get-tuple-element.37) | copy-start | bytes 7864324
  248.8 10.3 %copy-start.12 = (bf16[640,2048]{1,0:T(8,128)(2,1)S(1)}, bf16[640,2048]{1,0:T(8,128)(2,1)}, u32[]{:S(2)}) copy-start(bf16[640,2048]{1,0:T(8,128)(2,1)} %reshape.116) | copy-start | bytes 7864324
  248.8 10.3 %copy-start.19 = (bf16[2048,2048]{0,1:T(8,128)(2,1)S(1)}, bf16[2048,2048]{0,1:T(8,128)(2,1)}, u32[]{:S(2)}) copy-start(bf16[2048,2048]{0,1:T(8,128)(2,1)} %convolution_convert_fusion) | copy-start | bytes 25165828
  280.9 11.0 %copy-start.20 = (bf16[2048,2048]{1,0:T(8,128)(2,1)S(1)}, bf16[2048,2048]{1,0:T(8,128)(2,1)}, u32[]{:S(2)}) copy-start(bf16[2048,2048]{1,0:T(8,128)(2,1)} %get-tuple-element.19) | copy-start | bytes 25165828
  291.9 7.0 %copy-start.8 = (bf16[1,2048,640]{2,1,0:T(8,128)(2,1)S(1)}, bf16[1,2048,640]{2,1,0:T(8,128)(2,1)}, u32[]{:S(2)}) copy-start(bf16[1,2048,640]{2,1,0:T(8,128)(2,1)} %param.6) | copy-start | bytes 7864324
  318.8 10.8 %copy-start.6 = (bf16[2048,640]{0,1:T(8,128)(2,1)S(1)}, bf16[2048,640]{0,1:T(8,128)(2,1)}, u32[]{:S(2)}) copy-start(bf16[2048,640]{0,1:T(8,128)(2,1)} %copy-done.5) | copy-start | bytes 7864324
  318.9 10.8 %copy-start.14 = (bf16[640,2048]{1,0:T(8,128)(2,1)S(1)}, bf16[640,2048]{1,0:T(8,128)(2,1)}, u32[]{:S(2)}) copy-start(bf16[640,2048]{1,0:T(8,128)(2,1)} %reshape.117) | copy-start | bytes 7864324
  318.9 10.8 %copy-start.22 = (bf16[2048,640]{0,1:T(8,128)(2,1)S(1)}, bf16[2048,640]{0,1:T(8,128)(2,1)}, u32[]{:S(2)}) copy-start(bf16[2048,640]{0,1:T(8,128)(2,1)} %convolution_convert_fusion.9) | copy-start | bytes 7864324
  357.2 1.7 copy-start.4
  357.2 250.6 %reduce-scatter.3.cloned.1.call-start = ((), (), s32[]{:S(2)}) async-start(), calls=%async_computation.2 | async-start | bytes 8110080 | tf_op jit(solution)/shard_map/reduce_scatter | solution.py:29
  358.9 4.5 copy-start.11
  363.4 20.0 %copy-start.2 = (bf16[2048,640]{0,1:T(8,128)(2,1)}, bf16[2048,640]{0,1:T(8,128)(2,1)S(1)}, u32[]{:S(2)}) copy-start(bf16[2048,640]{0,1:T(8,128)(2,1)S(1)} %fusion.25) | copy-start | bytes 7864324
  363.4 23.2 %copy-start.1 = (bf16[1,2048,640]{1,2,0:T(8,128)(2,1)S(1)}, bf16[1,2048,640]{1,2,0:T(8,128)(2,1)}, u32[]{:S(2)}) copy-start(bf16[1,2048,640]{1,2,0:T(8,128)(2,1)} %copy-done) | copy-start | bytes 7864324
  363.4 23.2 %copy-start.18 = (f32[2048]{0:T(1024)S(1)}, f32[2048]{0:T(1024)}, u32[]{:S(2)}) copy-start(f32[2048]{0:T(1024)} %copy-done.17) | copy-start | bytes 24580
  383.4 3.2 copy-start.21
  438.0 9.8 %copy-start.10 = (bf16[640,2048]{1,0:T(8,128)(2,1)S(1)}, bf16[640,2048]{1,0:T(8,128)(2,1)}, u32[]{:S(2)}) copy-start(bf16[640,2048]{1,0:T(8,128)(2,1)} %reshape.112) | copy-start | bytes 7864324
  447.8 8.7 %copy-start.16 = (f32[2048]{0:T(1024)S(1)}, f32[2048]{0:T(1024)}, u32[]{:S(2)}) copy-start(f32[2048]{0:T(1024)} %copy-done.15) | copy-start | bytes 24580
  447.8 8.7 %copy-start.3 = (bf16[2048,640]{0,1:T(8,128)(2,1)S(1)}, bf16[2048,640]{0,1:T(8,128)(2,1)}, u32[]{:S(2)}) copy-start(bf16[2048,640]{0,1:T(8,128)(2,1)} %copy-done.2) | copy-start | bytes 7864324
Sparse Core Ops, SparseCore 0:
  12.7 77.7 all-gather.6
  93.5 73.8 all-gather.4
  357.3 122.3 reduce-scatter.4
  485.2 122.5 reduce-scatter.2
